TPU v7x, 512 devices: a whole 4x8x8 slice. The times are simulated.
512 devices in a mesh: row: 4 (over x), col: 4 (over z_lo), depth: 32 (over y, z_hi, core).
Axes of the slice: x: 4, y: 8, z: 8 (z_hi: 2, z_lo: 4; z = z_hi * 4 + z_lo), core: 2. Of those that a mesh axis runs over, the one named last changes fastest.
Arguments:
- orbitals: bfloat16 [2, 1024, 32, 4096], P(None, ('row', 'col'), 'depth'), may hold values from -20 to 20
- potential: float32 [32, 4096], P('depth'), may hold values from -6 to 6
Outputs:
- intersection: float32 [1024, 2, 1024], P(('row', 'depth'), None, 'col')
- applied: bfloat16 [2, 1024, 32, 4096], P(None, ('row', 'col'), 'depth')
All inputs are finite; a program needn't handle non-finite values.
Results may differ from a plain program's by a relative error of at most 0.001.
Values may be sent and summed in bfloat16 or wider, within the bound.
No kernel may reach another device: no remote copies, remote signals or barrier semaphores. Data moves between devices by JAX's collectives and lax.ppermute only.
A program may use at most 128 MiB of HBM per device.

v0:
```python
import jax
import jax.numpy as jnp
from jax import lax
from jax.sharding import PartitionSpec as P

NX = 64


def sent_to_all(x, axis):
    copies = jnp.broadcast_to(x, (lax.axis_size(axis), *x.shape))
    return lax.all_to_all(copies, axis, split_axis=0, concat_axis=0, tiled=True)


def in_order(pieces, dim):
    lengths = list(pieces.shape[1:])
    lengths[dim] *= pieces.shape[0]
    return jnp.moveaxis(pieces, 0, dim).reshape(lengths)


def gathered_copies(x, axis, dim):
    pieces = sent_to_all(x, axis)
    return in_order(pieces, dim)


def with_halo(block, sides, width):
    for axis, dim in sides:
        count = lax.axis_size(axis)
        forward = [(i, i + 1) for i in range(count - 1)]
        forward.append((count - 1, 0))
        backward = [(target, source) for source, target in forward]
        low = lax.ppermute(
            lax.slice_in_dim(block, block.shape[dim] - width, None, axis=dim), axis, forward
        )
        high = lax.ppermute(lax.slice_in_dim(block, 0, width, axis=dim), axis, backward)
        block = jnp.concatenate([low, block, high], axis=dim)
    return block


def cut_along(x, dim, size):
    before, after = (x.shape[:dim], x.shape[dim + 1 :])
    return jnp.moveaxis(x.reshape(*before, size, -1, *after), dim, 0)


def sum_at_owner(x, axis, dim):
    size = lax.axis_size(axis)
    pieces = lax.all_to_all(cut_along(x, dim, size), axis, 0, 0, tiled=True)
    return jnp.sum(pieces, axis=0)


def apply_operator(padded, potential):
    center = padded[:, :, 1:-1].astype(jnp.float32)
    below = padded[:, :, :-2].astype(jnp.float32)
    above = padded[:, :, 2:].astype(jnp.float32)
    flat_cells = center.shape[-1]
    xpos = jnp.arange(flat_cells) % NX
    yminus = jnp.roll(center, NX, axis=3)
    yplus = jnp.roll(center, -NX, axis=3)
    xminus = jnp.where(xpos == 0, jnp.roll(center, 1 - NX, axis=3), jnp.roll(center, 1, axis=3))
    xplus = jnp.where(
        xpos == NX - 1, jnp.roll(center, NX - 1, axis=3), jnp.roll(center, -1, axis=3)
    )
    lap = below + above + yminus + yplus + xminus + xplus - 6.0 * center
    return (-0.5 * lap + potential[None, None] * center).astype(jnp.bfloat16)


def contract(left, right):
    return lax.dot_general(
        left, right, (((1,), (1,)), ((), ())), preferred_element_type=jnp.float32
    )


def shards(orbitals, potential):
    parts, orbs, planes, cells = orbitals.shape
    flat = orbitals.reshape(parts, orbs, planes * cells)
    panel = lax.all_gather(flat, "col", axis=1, tiled=True)
    other = gathered_copies(flat, "row", 1)
    padded = with_halo(orbitals, (("depth", 2),), 1)
    applied = apply_operator(padded, potential)
    dvol = 1.0 / (planes * lax.axis_size("depth") * cells)
    tile_cols = other.shape[1]
    real_rows = panel[0]
    imag_rows = panel[1]
    sreal = contract(real_rows, other[0]) + contract(imag_rows, other[1])
    simag = contract(real_rows, other[1]) - contract(imag_rows, other[0])
    summed = sum_at_owner(dvol * jnp.concatenate([sreal, simag], axis=1), "depth", 0)
    intersection = summed.reshape(summed.shape[0], 2, tile_cols)
    intersection = lax.all_to_all(intersection, "col", split_axis=2, concat_axis=2, tiled=True)
    return (intersection, applied)


def solution(mesh):
    in_specs = (P(None, ("row", "col"), "depth", None), P("depth", None))
    out_specs = (P(("row", "depth"), None, "col"), P(None, ("row", "col"), "depth", None))
    return jax.shard_map(shards, mesh=mesh, in_specs=in_specs, out_specs=out_specs, check_vma=False)
```

profile of v0, /device:TPU:10, one launch (start us, length us, event | category | flops | bytes accessed | tf_op | source)
XLA Modules:
  0.0 205.3 jit_solution(4994023229630989519)
XLA Ops:
  7.2 0.0 all-gather.3.cloned.1.call-start
  7.2 0.7 all-gather.3.cloned.1.call-update
  7.9 3.7 %broadcast_in_dim.11 = bf16[4,2,64,4096]{3,2,1,0:T(8,128)(2,1)} broadcast(bf16[2,64,4096]{2,1,0:T(8,128)(2,1)} %bitcast.31), dimensions={1,2,3} | broadcast | bytes 5242880 | tf_op jit(solution)/shard_map/broadcast_in_dim | solution.py:10
  11.6 0.0 copy-start
  11.6 5.5 %all-to-all-start = ((bf16[4,2,64,4096]{3,2,1,0:T(8,128)(2,1)}), bf16[4,2,64,4096]{3,2,1,0:T(8,128)(2,1)}, u32[]{:S(2)}, u32[]{:S(2)}) async-start(bf16[4,2,64,4096]{3,2,1,0:T(8,128)(2,1)} %broadcast_in_dim.11), calls=%async_computation | async-start | bytes 8388608 | tf_op jit(solution)/shard_map/all_to_all | solution.py:11
  17.1 0.0 copy-done
  17.1 1.9 collective-permute-start
  19.0 10.0 %collective-permute-start.1 = (bf16[2,64,1,4096]{3,1,2,0:T(8,128)(2,1)S(1)}, bf16[2,64,1,4096]{3,1,2,0:T(8,128)(2,1)}, u32[]{:S(2)}, u32[]{:S(2)}) collective-permute-start(bf16[2,64,1,4096]{3,1,2,0:T(8,128)(2,1)S(1)} %copy-done), channel_id=1, source_target_pairs={{1,0},{2,1},{3,2},{4,3},{5,4},{6,5},{7,6},{8,7},{9,8},{10,9},{11,1... | collective-permute-start | bytes 3145736 | tf_op jit(solution)/shard_map/ppermute | solution.py:34
  29.0 0.6 fusion.17
  29.6 0.1 fusion.26
  29.7 0.7 fusion.23
  30.4 0.7 fusion.22
  31.1 1.8 fusion.24
  32.9 2.4 %fusion.25 = (f32[2,64,1,4032]{3,1,2,0:T(8,128)}, f32[2,64,1,4032]{3,1,2,0:T(8,128)}) fusion(bf16[2,64,1,4096]{3,1,2,0:T(8,128)(2,1)S(1)} %copy-done), kind=kLoop, calls=%fused_computation.33 | loop fusion | bytes 8257536 | tf_op jit(solution)/shard_map/jit(_roll_static)/slice | solution.py:57
  35.3 29.5 %all-to-all-done = bf16[4,2,64,4096]{3,2,1,0:T(8,128)(2,1)} async-done(((bf16[4,2,64,4096]{3,2,1,0:T(8,128)(2,1)}), bf16[4,2,64,4096]{3,2,1,0:T(8,128)(2,1)}, u32[]{:S(2)}, u32[]{:S(2)}) %all-to-all-start) | async-done | bytes 4194336 | tf_op jit(solution)/shard_map/all_to_all | solution.py:11
  64.8 4.7 %fusion.20 = (bf16[1,4,64,4096]{3,2,0,1:T(8,128)(2,1)}, bf16[1,4,64,4096]{3,2,0,1:T(8,128)(2,1)}) fusion(bf16[2,4,64,4096]{3,2,0,1:T(8,128)(2,1)} %bitcast.2), kind=kLoop, calls=%fused_computation.28 | loop fusion | bytes 8388608 | tf_op jit(solution)/shard_map/slice | solution.py:83
  69.5 74.9 %all-gather.3.cloned.1.call-done = bf16[2,256,1,4096]{3,1,2,0:T(8,128)(2,1)} async-done(((bf16[2,64,1,4096]{3,1,2,0:T(8,128)(2,1)}), bf16[2,256,1,4096]{3,1,2,0:T(8,128)(2,1)}) %all-gather.3.cloned.1.call-update) | async-done | bytes 4194320 | tf_op jit(solution)/shard_map/all_gather | solution.py:75
  144.4 0.0 copy-start.2
  144.4 3.1 %fusion.7 = f32[256,256]{1,0:T(8,128)S(1)} fusion(bf16[256,4096]{1,0:T(8,128)(2,1)} %bitcast.32, bf16[2,256,1,4096]{3,1,2,0:T(8,128)(2,1)} %all-gather.3.cloned.1.call-done), kind=kOutput, calls=%fused_computation.12 | convolution fusion | flops 536870912 | bytes 4456448 | tf_op jit(solution)/shard_map/dot_general | solution.py:67
  147.5 0.0 copy-done.2
  147.5 0.0 copy-start.3
  147.5 2.5 %fusion.8 = f32[256,256]{1,0:T(8,128)S(1)} fusion(bf16[256,4096]{1,0:T(8,128)(2,1)S(1)} %bitcast.34, bf16[2,256,1,4096]{3,1,2,0:T(8,128)(2,1)} %all-gather.3.cloned.1.call-done), kind=kOutput, calls=%fused_computation.13 | convolution fusion | flops 536870912 | bytes 4456448 | tf_op jit(solution)/shard_map/dot_general | solution.py:67
  150.0 0.3 copy-done.3
  150.4 0.0 copy-start.1
  150.4 0.7 fusion.14
  151.1 0.8 copy-done.1
  151.9 0.7 fusion.12
  152.7 0.9 maximum_multiply_fusion
  153.6 9.2 %all-to-all-start.1 = ((f32[32,8,512]{2,1,0:T(8,128)}), f32[32,8,512]{2,1,0:T(8,128)}, u32[]{:S(2)}, u32[]{:S(2)}) async-start(f32[32,8,512]{2,1,0:T(8,128)} %maximum_multiply_fusion), calls=%async_computation.1 | async-start | bytes 1048576 | tf_op jit(solution)/shard_map/all_to_all | solution.py:46
  162.8 2.4 %fusion.21 = (f32[2,64,1,4095]{3,1,2,0:T(8,128)}, f32[2,64,1,4095]{3,1,2,0:T(8,128)}) fusion(bf16[2,64,1,4096]{3,1,2,0:T(8,128)(2,1)S(1)} %copy-done), kind=kLoop, calls=%fused_computation.29 | loop fusion | bytes 8386560 | tf_op jit(solution)/shard_map/jit(_roll_static)/slice | solution.py:60
  165.2 17.6 %all-to-all-done.1 = f32[32,8,512]{2,1,0:T(8,128)} async-done(((f32[32,8,512]{2,1,0:T(8,128)}), f32[32,8,512]{2,1,0:T(8,128)}, u32[]{:S(2)}, u32[]{:S(2)}) %all-to-all-start.1) | async-done | bytes 524320 | tf_op jit(solution)/shard_map/all_to_all | solution.py:46
  182.8 1.1 reduce_sum.9
  183.9 0.2 copy.7
  184.1 1.0 reshape.132
  185.1 4.2 %all-to-all-start.2 = ((f32[4,1,1024]{2,1,0:T(1,128)}), f32[4,1,1024]{2,1,0:T(1,128)S(1)}, u32[]{:S(2)}, u32[]{:S(2)}) async-start(f32[4,1,1024]{2,1,0:T(1,128)} %reshape.132), calls=%async_computation.2 | async-start | bytes 32768 | tf_op jit(solution)/shard_map/all_to_all | solution.py:87
  189.2 0.0 collective-permute-done
  189.2 0.0 collective-permute-done.1
  189.2 6.8 %fusion.6 = bf16[2,64,1,4096]{3,1,2,0:T(8,128)(2,1)} fusion(f32[2,64,1,4032]{3,1,2,0:T(8,128)} %get-tuple-element.19, f32[2,64,1,64]{3,1,2,0:T(8,128)S(1)} %get-tuple-element.21, f32[2,64,1,64]{3,1,2,0:T(8,128)S(1)} %get-tuple-element.20, f32[2,64,1,4032]{3,1,2,0:T(8,128)} %get-tuple-element.18, f32[2,64,1,63]{3,1,2,0:T(8,128)} %get-tuple-element.15, ...), kind=kLoop, calls=%fused_computation.9 | loop fusion | flops 11534336 | bytes 16801792 | tf_op jit(solution)/shard_map/convert_element_type | solution.py:63
  196.1 0.0 all-to-all-done.2
  196.1 0.5 broadcast.23
  196.6 0.7 reduce
  197.3 0.4 reshape.133
  197.7 0.7 copy.8
  (1 shorter events, 0.0 us)
Async XLA Ops:
  7.2 137.2 %all-gather.3.cloned.1.call-start = ((), (), s32[]{:S(2)}) async-start(), calls=%async_computation.3 | async-start | bytes 5242880 | tf_op jit(solution)/shard_map/all_gather | solution.py:75
  11.6 5.5 %copy-start = (bf16[2,64,1,4096]{3,1,2,0:T(8,128)(2,1)S(1)}, bf16[2,64,1,4096]{3,1,2,0:T(8,128)(2,1)}, u32[]{:S(2)}) copy-start(bf16[2,64,1,4096]{3,1,2,0:T(8,128)(2,1)} %param.2) | copy-start | bytes 3145732
  11.6 53.2 %all-to-all-start = ((bf16[4,2,64,4096]{3,2,1,0:T(8,128)(2,1)}), bf16[4,2,64,4096]{3,2,1,0:T(8,128)(2,1)}, u32[]{:S(2)}, u32[]{:S(2)}) async-start(bf16[4,2,64,4096]{3,2,1,0:T(8,128)(2,1)} %broadcast_in_dim.11), calls=%async_computation | async-start | bytes 8388608 | tf_op jit(solution)/shard_map/all_to_all | solution.py:11
  17.1 172.2 %collective-permute-start = (bf16[2,64,1,4096]{3,1,2,0:T(8,128)(2,1)S(1)}, bf16[2,64,1,4096]{3,1,2,0:T(8,128)(2,1)}, u32[]{:S(2)}, u32[]{:S(2)}) collective-permute-start(bf16[2,64,1,4096]{3,1,2,0:T(8,128)(2,1)S(1)} %copy-done), channel_id=1, source_target_pairs={{0,1},{1,2},{2,3},{3,4},{4,5},{5,6},{6,7},{7,8},{8,9},{9,10},{10,1... | collective-permute-start | bytes 3145736 | tf_op jit(solution)/shard_map/ppermute | solution.py:31
  19.0 170.2 %collective-permute-start.1 = (bf16[2,64,1,4096]{3,1,2,0:T(8,128)(2,1)S(1)}, bf16[2,64,1,4096]{3,1,2,0:T(8,128)(2,1)}, u32[]{:S(2)}, u32[]{:S(2)}) collective-permute-start(bf16[2,64,1,4096]{3,1,2,0:T(8,128)(2,1)S(1)} %copy-done), channel_id=1, source_target_pairs={{1,0},{2,1},{3,2},{4,3},{5,4},{6,5},{7,6},{8,7},{9,8},{10,9},{11,1... | collective-permute-start | bytes 3145736 | tf_op jit(solution)/shard_map/ppermute | solution.py:34
  144.4 3.1 %copy-start.2 = (bf16[1,4,64,4096]{3,2,0,1:T(8,128)(2,1)S(1)}, bf16[1,4,64,4096]{3,2,0,1:T(8,128)(2,1)}, u32[]{:S(2)}) copy-start(bf16[1,4,64,4096]{3,2,0,1:T(8,128)(2,1)} %get-tuple-element.8) | copy-start | bytes 6291460
  147.5 2.8 %copy-start.3 = (bf16[2,256,1,4096]{3,1,2,0:T(8,128)(2,1)S(1)}, bf16[2,256,1,4096]{3,1,2,0:T(8,128)(2,1)}, u32[]{:S(2)}) copy-start(bf16[2,256,1,4096]{3,1,2,0:T(8,128)(2,1)} %all-gather.3.cloned.1.call-done) | copy-start | bytes 12582916
  150.4 1.6 copy-start.1
  153.6 29.2 %all-to-all-start.1 = ((f32[32,8,512]{2,1,0:T(8,128)}), f32[32,8,512]{2,1,0:T(8,128)}, u32[]{:S(2)}, u32[]{:S(2)}) async-start(f32[32,8,512]{2,1,0:T(8,128)} %maximum_multiply_fusion), calls=%async_computation.1 | async-start | bytes 1048576 | tf_op jit(solution)/shard_map/all_to_all | solution.py:46
  185.1 11.0 %all-to-all-start.2 = ((f32[4,1,1024]{2,1,0:T(1,128)}), f32[4,1,1024]{2,1,0:T(1,128)S(1)}, u32[]{:S(2)}, u32[]{:S(2)}) async-start(f32[4,1,1024]{2,1,0:T(1,128)} %reshape.132), calls=%async_computation.2 | async-start | bytes 32768 | tf_op jit(solution)/shard_map/all_to_all | solution.py:87
Sparse Core Ops, SparseCore 0:
  10.1 134.2 all-gather.2
where the time goes:
time: 206 us; the launch traced here: 205 us
  waiting for transfers between devices  123 us (60%)
  starting transfers between devices  30.7 us (15%)
  local copies, waits for them, and re-layouts  20.6 us (10%)
  between operations  14.1 us (7%)
  other arithmetic  10.1 us (5%)
  matrix products  7.07 us (3%)
    all_gather x1, waiting for transfers between devices, shards(): panel = lax.all_gather(flat, 'col', axis=1, tiled=True)  74.9 us
    all_to_all x1, waiting for transfers between devices, sent_to_all(): return lax.all_to_all(copies, axis, split_axis=0, concat_axis=0, tiled=True)  29.5 us
    all_to_all x1, waiting for transfers between devices, sum_at_owner(): pieces = lax.all_to_all(cut_along(x, dim, size), axis, 0, 0, tiled=True)  17.6 us
    ppermute x1, starting transfers between devices, with_halo(): lax.ppermute(lax.slice_in_dim(block, 0, width, axis=dim), axis, backward)  9.96 us
    all_to_all x1, starting transfers between devices, sum_at_owner(): pieces = lax.all_to_all(cut_along(x, dim, size), axis, 0, 0, tiled=True)  9.19 us
    dot_general x4, matrix products, contract(): lax.dot_general(left, right, (((1,), (1,)), ((), ())), preferred_element_...  7.07 us
    convert_element_type x1, other arithmetic, apply_operator(): return (-0.5 * lap + potential[None, None] * center).astype(jnp.bfloat16)  6.82 us
    all_to_all x1, starting transfers between devices, sent_to_all(): return lax.all_to_all(copies, axis, split_axis=0, concat_axis=0, tiled=True)  5.47 us
  transfers between devices with their start and end apart: 6, of which 3 were waited for; matrix products, arithmetic and copies ran while one was open for 17% of the time, Pallas kernels for 0%

commit v1 on v0

--- a/solution.py
+++ b/solution.py
@@ -72,7 +72,9 @@
 def shards(orbitals, potential):
     parts, orbs, planes, cells = orbitals.shape
     flat = orbitals.reshape(parts, orbs, planes * cells)
-    panel = lax.all_gather(flat, "col", axis=1, tiled=True)
+    panel = jnp.concatenate(
+        lax.all_to_all(jnp.stack([flat] * lax.axis_size("col")), "col", 0, 0), axis=1
+    )
     other = gathered_copies(flat, "row", 1)
     padded = with_halo(orbitals, (("depth", 2),), 1)
     applied = apply_operator(padded, potential)

time: 206 us -> 259 us (1.26)
  the two profiles are of different devices: /device:TPU:10 before, /device:TPU:8 now
where the time goes in v1:
time: 259 us; the launch traced here: 258 us
  waiting for transfers between devices  134 us (52%)
  blocking collectives  53 us (20%)
  starting transfers between devices  35 us (14%)
  local copies, waits for them, and re-layouts  21.9 us (8%)
  other arithmetic  10.1 us (4%)
  matrix products  2.96 us (1%)
    all_to_all x1, waiting for transfers between devices, shards(): lax.all_to_all(jnp.stack([flat] * lax.axis_size('col')), 'col', 0, 0)  117 us
    all_to_all x1, blocking collectives, sent_to_all(): return lax.all_to_all(copies, axis, split_axis=0, concat_axis=0, tiled=True)  53 us
    all_to_all x1, waiting for transfers between devices, sum_at_owner(): pieces = lax.all_to_all(cut_along(x, dim, size), axis, 0, 0, tiled=True)  17.6 us
    all_to_all x1, starting transfers between devices, sum_at_owner(): pieces = lax.all_to_all(cut_along(x, dim, size), axis, 0, 0, tiled=True)  14 us
    ppermute x1, starting transfers between devices, with_halo(): lax.ppermute(lax.slice_in_dim(block, 0, width, axis=dim), axis, backward)  8.45 us
    all_to_all x1, starting transfers between devices, shards(): lax.all_to_all(jnp.stack([flat] * lax.axis_size('col')), 'col', 0, 0)  7.39 us
    convert_element_type x1, other arithmetic, apply_operator(): return (-0.5 * lap + potential[None, None] * center).astype(jnp.bfloat16)  6.82 us
    unnamed x13, local copies, waits for them, and re-layouts  6.03 us
  transfers between devices with their start and end apart: 5, of which 2 were waited for; matrix products, arithmetic and copies ran while one was open for 10% of the time, Pallas kernels for 0%

profile of v1, /device:TPU:8, one launch (start us, length us, event | category | flops | bytes accessed | tf_op | source)
XLA Modules:
  0.0 258.0 jit_solution(11956113015463955618)
XLA Ops:
  0.6 1.7 stack.3
  2.4 0.0 copy-start.1
  2.4 2.0 copy-done.1
  4.3 53.0 %all_to_all.20 = bf16[4,2,64,4096]{3,2,1,0:T(8,128)(2,1)} all-to-all(bf16[4,2,64,4096]{3,2,1,0:T(8,128)(2,1)S(1)} %stack.3), channel_id=1, replica_groups=mesh['row'=4,'col'=4,'depth'=32] {'row'}, dimensions={0} | all-to-all | bytes 8388608 | tf_op jit(solution)/shard_map/all_to_all | solution.py:11
  57.3 0.0 copy-start
  57.3 7.4 %all-to-all-start = ((bf16[4,2,64,4096]{3,2,1,0:T(8,128)(2,1)}), bf16[4,2,64,4096]{3,2,1,0:T(8,128)(2,1)}, u32[]{:S(2)}, u32[]{:S(2)}) async-start(bf16[4,2,64,4096]{3,2,1,0:T(8,128)(2,1)} %copy-done.1), calls=%async_computation | async-start | bytes 8388608 | tf_op jit(solution)/shard_map/all_to_all | solution.py:76
  64.7 0.0 copy-done
  64.7 1.9 collective-permute-start
  66.6 8.4 %collective-permute-start.1 = (bf16[2,64,1,4096]{3,1,2,0:T(8,128)(2,1)S(1)}, bf16[2,64,1,4096]{3,1,2,0:T(8,128)(2,1)}, u32[]{:S(2)}, u32[]{:S(2)}) collective-permute-start(bf16[2,64,1,4096]{3,1,2,0:T(8,128)(2,1)S(1)} %copy-done), channel_id=1, source_target_pairs={{1,0},{2,1},{3,2},{4,3},{5,4},{6,5},{7,6},{8,7},{9,8},{10,9},{11,1... | collective-permute-start | bytes 3145736 | tf_op jit(solution)/shard_map/ppermute | solution.py:34
  75.1 0.6 fusion.11
  75.7 0.1 fusion.21
  75.8 0.7 fusion.18
  76.5 0.7 fusion.17
  77.2 2.4 fusion.19
  79.6 0.0 copy-start.3
  79.6 2.6 %fusion.20 = (f32[2,64,1,4032]{3,1,2,0:T(8,128)}, f32[2,64,1,4032]{3,1,2,0:T(8,128)}) fusion(bf16[2,64,1,4096]{3,1,2,0:T(8,128)(2,1)S(1)} %copy-done), kind=kLoop, calls=%fused_computation.28 | loop fusion | bytes 8257536 | tf_op jit(solution)/shard_map/jit(_roll_static)/slice | solution.py:57
  82.2 1.1 copy-done.3
  83.3 1.8 fusion.14
  85.1 116.7 %all-to-all-done = bf16[4,2,64,4096]{3,2,1,0:T(8,128)(2,1)} async-done(((bf16[4,2,64,4096]{3,2,1,0:T(8,128)(2,1)}), bf16[4,2,64,4096]{3,2,1,0:T(8,128)(2,1)}, u32[]{:S(2)}, u32[]{:S(2)}) %all-to-all-start) | async-done | bytes 4194336 | tf_op jit(solution)/shard_map/all_to_all | solution.py:76
  201.8 2.7 %fusion.15 = (bf16[1,4,64,4096]{3,2,0,1:T(8,128)(2,1)S(1)}, bf16[1,4,64,4096]{3,2,0,1:T(8,128)(2,1)S(1)}) fusion(bf16[2,4,64,4096]{3,2,0,1:T(8,128)(2,1)} %bitcast.1), kind=kLoop, calls=%fused_computation.23 | loop fusion | bytes 8388608 | tf_op jit(solution)/shard_map/slice | solution.py:84
  204.5 0.0 copy-start.2
  204.5 0.7 fusion.23
  205.2 0.8 copy-done.2
  206.1 0.7 fusion.22
  206.8 0.7 fusion.7
  207.6 0.7 fusion.8
  208.3 0.9 maximum_multiply_fusion
  209.2 14.0 %all-to-all-start.2 = ((f32[32,8,512]{2,1,0:T(8,128)}), f32[32,8,512]{2,1,0:T(8,128)}, u32[]{:S(2)}, u32[]{:S(2)}) async-start(f32[32,8,512]{2,1,0:T(8,128)} %maximum_multiply_fusion), calls=%async_computation.2 | async-start | bytes 1048576 | tf_op jit(solution)/shard_map/all_to_all | solution.py:46
  223.2 0.0 copy-start.4
  223.2 2.4 fusion.16
  225.7 17.6 %all-to-all-done.2 = f32[32,8,512]{2,1,0:T(8,128)} async-done(((f32[32,8,512]{2,1,0:T(8,128)}), f32[32,8,512]{2,1,0:T(8,128)}, u32[]{:S(2)}, u32[]{:S(2)}) %all-to-all-start.2) | async-done | bytes 524320 | tf_op jit(solution)/shard_map/all_to_all | solution.py:46
  243.3 1.1 reduce_sum.9
  244.4 0.2 copy.7
  244.5 1.0 reshape.135
  245.5 3.3 %all-to-all-start.3 = ((f32[4,1,1024]{2,1,0:T(1,128)}), f32[4,1,1024]{2,1,0:T(1,128)S(1)}, u32[]{:S(2)}, u32[]{:S(2)}) async-start(f32[4,1,1024]{2,1,0:T(1,128)} %reshape.135), calls=%async_computation.3 | async-start | bytes 32768 | tf_op jit(solution)/shard_map/all_to_all | solution.py:89
  248.8 0.0 collective-permute-done
  248.8 0.0 collective-permute-done.1
  248.8 0.0 copy-done.4
  248.8 6.8 %fusion.6 = bf16[2,64,1,4096]{3,1,2,0:T(8,128)(2,1)} fusion(f32[2,64,1,4032]{3,1,2,0:T(8,128)} %get-tuple-element.21, f32[2,64,1,64]{3,1,2,0:T(8,128)S(1)} %get-tuple-element.23, f32[2,64,1,64]{3,1,2,0:T(8,128)S(1)} %get-tuple-element.22, f32[2,64,1,4032]{3,1,2,0:T(8,128)} %get-tuple-element.20, f32[2,64,1,63]{3,1,2,0:T(8,128)} %get-tuple-element.17, ...), kind=kLoop, calls=%fused_computation.7 | loop fusion | flops 11534336 | bytes 16801792 | tf_op jit(solution)/shard_map/convert_element_type | solution.py:63
  255.6 0.0 all-to-all-done.3
  255.7 0.5 broadcast.24
  256.2 0.7 reduce
  256.9 0.4 reshape.136
  257.3 0.7 copy.8
  (1 shorter events, 0.0 us)
Async XLA Ops:
  2.4 2.0 copy-start.1
  57.3 7.4 %copy-start = (bf16[2,64,1,4096]{3,1,2,0:T(8,128)(2,1)S(1)}, bf16[2,64,1,4096]{3,1,2,0:T(8,128)(2,1)}, u32[]{:S(2)}) copy-start(bf16[2,64,1,4096]{3,1,2,0:T(8,128)(2,1)} %param.2) | copy-start | bytes 3145732
  57.3 144.4 %all-to-all-start = ((bf16[4,2,64,4096]{3,2,1,0:T(8,128)(2,1)}), bf16[4,2,64,4096]{3,2,1,0:T(8,128)(2,1)}, u32[]{:S(2)}, u32[]{:S(2)}) async-start(bf16[4,2,64,4096]{3,2,1,0:T(8,128)(2,1)} %copy-done.1), calls=%async_computation | async-start | bytes 8388608 | tf_op jit(solution)/shard_map/all_to_all | solution.py:76
  64.7 184.1 %collective-permute-start = (bf16[2,64,1,4096]{3,1,2,0:T(8,128)(2,1)S(1)}, bf16[2,64,1,4096]{3,1,2,0:T(8,128)(2,1)}, u32[]{:S(2)}, u32[]{:S(2)}) collective-permute-start(bf16[2,64,1,4096]{3,1,2,0:T(8,128)(2,1)S(1)} %copy-done), channel_id=1, source_target_pairs={{0,1},{1,2},{2,3},{3,4},{4,5},{5,6},{6,7},{7,8},{8,9},{9,10},{10,1... | collective-permute-start | bytes 3145736 | tf_op jit(solution)/shard_map/ppermute | solution.py:31
  66.6 182.2 %collective-permute-start.1 = (bf16[2,64,1,4096]{3,1,2,0:T(8,128)(2,1)S(1)}, bf16[2,64,1,4096]{3,1,2,0:T(8,128)(2,1)}, u32[]{:S(2)}, u32[]{:S(2)}) collective-permute-start(bf16[2,64,1,4096]{3,1,2,0:T(8,128)(2,1)S(1)} %copy-done), channel_id=1, source_target_pairs={{1,0},{2,1},{3,2},{4,3},{5,4},{6,5},{7,6},{8,7},{9,8},{10,9},{11,1... | collective-permute-start | bytes 3145736 | tf_op jit(solution)/shard_map/ppermute | solution.py:34
  79.6 3.7 %copy-start.3 = (bf16[4,2,64,4096]{3,2,1,0:T(8,128)(2,1)S(1)}, bf16[4,2,64,4096]{3,2,1,0:T(8,128)(2,1)}, u32[]{:S(2)}) copy-start(bf16[4,2,64,4096]{3,2,1,0:T(8,128)(2,1)} %all_to_all.20) | copy-start | bytes 12582916
  204.5 1.6 copy-start.2
  209.2 34.1 %all-to-all-start.2 = ((f32[32,8,512]{2,1,0:T(8,128)}), f32[32,8,512]{2,1,0:T(8,128)}, u32[]{:S(2)}, u32[]{:S(2)}) async-start(f32[32,8,512]{2,1,0:T(8,128)} %maximum_multiply_fusion), calls=%async_computation.2 | async-start | bytes 1048576 | tf_op jit(solution)/shard_map/all_to_all | solution.py:46
  223.2 25.6 %copy-start.4 = (f32[2,64,1,4033]{3,1,2,0:T(8,128)S(1)}, f32[2,64,1,4033]{3,1,2,0:T(8,128)}, u32[]{:S(2)}) copy-start(f32[2,64,1,4033]{3,1,2,0:T(8,128)} %get-tuple-element.18) | copy-start | bytes 6194692
  245.5 10.1 %all-to-all-start.3 = ((f32[4,1,1024]{2,1,0:T(1,128)}), f32[4,1,1024]{2,1,0:T(1,128)S(1)}, u32[]{:S(2)}, u32[]{:S(2)}) async-start(f32[4,1,1024]{2,1,0:T(1,128)} %reshape.135), calls=%async_computation.3 | async-start | bytes 32768 | tf_op jit(solution)/shard_map/all_to_all | solution.py:89
